TPU v7x, 512 devices: a whole 4x4x16 slice. The times are simulated.
512 devices in a mesh: rows: 32 (over x_lo, z), ka: 16 (over x_hi, y, core).
Axes of the slice: x: 4 (x_hi: 2, x_lo: 2; x = x_hi * 2 + x_lo), y: 4, z: 16, core: 2. Of those that a mesh axis runs over, the one named last changes fastest.
Arguments:
- pair_repr: bfloat16 [512, 512, 128], P('rows', 'ka'), may hold values from -6 to 6
- pair_mask: int32 [512, 512], P('rows', 'ka'), may hold values 0 or 1
- ln_gain: float32 [128], replicated, may hold values from 0.1 to 1.9
- ln_bias: float32 [128], replicated, may hold values from -3 to 3
- w_proj: bfloat16 [128, 256], replicated, may hold values from -0.5 to 0.5
- w_gate: bfloat16 [128, 256], replicated, may hold values from -0.5 to 0.5
- w_out_gate: bfloat16 [128, 128], replicated, may hold values from -0.5 to 0.5
- out_gain: float32 [128], replicated, may hold values from 0.1 to 1.9
- out_bias: float32 [128], replicated, may hold values from -3 to 3
- w_out: bfloat16 [128, 128], replicated, may hold values from -0.5 to 0.5
Outputs:
- update: bfloat16 [512, 512, 128], P('rows', 'ka')
All inputs are finite; a program needn't handle non-finite values. No bound on the sum of `pair_mask` on one device may be relied on, other than what follows from the above.
Results may differ from a plain program's by a relative error of at most 0.015.
Values may be sent and summed in bfloat16 or wider, within the bound.
A program may use at most 64 MiB of HBM per device.

v0:
```python
import jax
import jax.numpy as jnp
from jax import lax
from jax.sharding import Mesh
from jax.sharding import PartitionSpec as P

ROWS = ("rows_0", "rows_1")
KA = ("ka_0", "ka_1", "ka_2")


def joined_along(blocks, dim):
    blocks = jnp.moveaxis(blocks, 0, dim)
    dims = blocks.shape
    return blocks.reshape(*dims[:dim], dims[dim] * dims[dim + 1], *dims[dim + 2 :])


def stacked_from(array, axes, order):
    blocks = array[None]
    for k in order:
        blocks = lax.all_gather(blocks, axes[k], axis=0, tiled=True)
    carried = [lax.axis_size(axes[k]) for k in reversed(order)]
    blocks = blocks.reshape(*carried, *array.shape)
    turned = sorted(range(len(order)), key=lambda place: order[len(order) - 1 - place])
    return blocks.transpose(*turned, *range(len(order), blocks.ndim)).reshape(-1, *array.shape)


def whole_of(array, axes, order, dim):
    return joined_along(stacked_from(array, axes, order), dim)


def split_up(array, dim, count):
    dims = array.shape
    blocks = array.reshape(*dims[:dim], count, dims[dim] // count, *dims[dim + 1 :])
    return jnp.moveaxis(blocks, dim, 0)


def sum_at_owner(array, axis, dim):
    blocks = split_up(array, dim, lax.axis_size(axis))
    arrived = lax.all_to_all(blocks, axis, split_axis=0, concat_axis=0, tiled=True)
    return arrived.astype(jnp.float32).sum(axis=0)


def sum_in_two_steps(array, axes, dim):
    far, near = axes
    blocks = split_up(array, dim, lax.axis_size(far))
    nearer = sum_at_owner(blocks, near, dim + 1)
    arrived = lax.all_to_all(
        nearer.astype(jnp.bfloat16), far, split_axis=0, concat_axis=0, tiled=True
    )
    return arrived.astype(jnp.float32).sum(axis=0)


def layer_norm(values, gain_vec, bias_vec):
    center = jnp.mean(values, axis=-1, keepdims=True)
    deviate = values - center
    spread = jnp.mean(deviate * deviate, axis=-1, keepdims=True)
    return deviate * lax.rsqrt(spread + 1e-05) * gain_vec + bias_vec


def panel_sums(left_edge, right_edge):
    return jnp.einsum(
        "ikh,jkh->ijh",
        left_edge,
        whole_of(right_edge, ROWS, (0, 1), 0),
        preferred_element_type=jnp.float32,
    )


def body(
    pair_repr, pair_mask, ln_gain, ln_bias, w_proj, w_gate, w_out_gate, out_gain, out_bias, w_out
):
    row_count, col_count, chans = pair_repr.shape
    hidden = w_out.shape[0]
    normed = layer_norm(pair_repr.astype(jnp.float32), ln_gain, ln_bias).astype(jnp.bfloat16)
    flat_rows = normed.reshape(row_count * col_count, chans)
    projected = jnp.dot(flat_rows, w_proj, preferred_element_type=jnp.float32)
    gate_logits = jnp.dot(flat_rows, w_gate, preferred_element_type=jnp.float32)
    mask_col = pair_mask.reshape(row_count * col_count, 1).astype(jnp.float32)
    edges = (jax.nn.sigmoid(gate_logits) * projected * mask_col).astype(jnp.bfloat16)
    edges = edges.reshape(row_count, col_count, 2 * hidden)
    left_edge = edges[:, :, :hidden]
    right_edge = edges[:, :, hidden:]
    partial_sums = panel_sums(left_edge, right_edge)
    triangle = sum_in_two_steps(partial_sums.astype(jnp.bfloat16), (("ka_0", "ka_1"), "ka_2"), 1)
    tri_normed = layer_norm(triangle, out_gain, out_bias).astype(jnp.bfloat16)
    out_gate = jax.nn.sigmoid(jnp.dot(flat_rows, w_out_gate, preferred_element_type=jnp.float32))
    projected_out = jnp.dot(
        tri_normed.reshape(row_count * col_count, hidden), w_out, preferred_element_type=jnp.float32
    )
    return (out_gate * projected_out).astype(jnp.bfloat16).reshape(row_count, col_count, chans)


def solution(mesh):
    torus = Mesh(mesh.devices.reshape(2, 16, 2, 4, 2), ("rows_0", "rows_1", "ka_0", "ka_1", "ka_2"))
    placed = (P(ROWS, KA, None), P(ROWS, KA), P(), P(), P(), P(), P(), P(), P(), P())
    return jax.shard_map(
        body, mesh=torus, in_specs=placed, out_specs=P(ROWS, KA, None), check_vma=False
    )
```

profile of v0, /device:TPU:32, one launch (start us, length us, event | category | flops | bytes accessed | tf_op | source)
XLA Modules:
  0.0 160.8 jit_solution(4884521978984217984)
XLA Ops:
  6.5 0.0 copy-start
  6.5 0.0 all-gather.3.cloned.1.call-start
  6.5 1.1 convert_reduce_fusion.2
  7.6 1.2 fusion.11
  8.8 0.7 convert_element_type.40
  9.5 0.1 convert_element_type.41
  9.6 1.1 fusion.14
  10.7 0.0 copy-done
  10.7 0.3 fusion.2
  11.0 1.1 fusion.4
  12.2 6.0 %all-gather = bf16[32,32,128]{2,1,0:T(8,128)(2,1)} all-gather(bf16[16,32,128]{2,1,0:T(8,128)(2,1)S(1)} %get-tuple-element.7), channel_id=2, replica_groups=mesh['rows_0'=2,'rows_1'=16,'ka_0'=2,'ka_1'=4,'ka_2'=2] {'rows_0'}, dimensions={0}, use_global_device_ids=true | all-gather | bytes 393216 | tf_op jit(solution)/shard_map/all_gather | solution.py:20
  18.2 0.0 all-gather.3.cloned.1.call-update
  18.2 0.4 copy.30
  18.6 81.8 %all-gather.3.cloned.1.call-done = bf16[32,16,32,128]{3,2,1,0:T(8,128)(2,1)} async-done(((bf16[2,16,32,128]{3,2,1,0:T(8,128)(2,1)}), bf16[32,16,32,128]{3,2,1,0:T(8,128)(2,1)}) %all-gather.3.cloned.1.call-update) | async-done | bytes 4194320 | tf_op jit(solution)/shard_map/all_gather | solution.py:20
  100.4 5.3 %copy.23 = bf16[2,16,16,32,128]{4,3,2,1,0:T(8,128)(2,1)} copy(bf16[2,16,16,32,128]{4,3,2,0,1:T(8,128)(2,1)} %bitcast.39) | data formatting | bytes 8388608 | tf_op jit(solution)/shard_map/transpose | solution.py:24
  105.8 8.6 %copy.25 = bf16[512,32,128]{0,1,2:T(8,128)(2,1)} copy(bf16[512,32,128]{2,1,0:T(8,128)(2,1)} %bitcast.37) | data formatting | bytes 8388608 | tf_op jit(solution)/shard_map/reshape;reshape | solution.py:14
  114.4 2.9 %convert_bitcast_fusion = bf16[16,512,128]{1,0,2:T(8,128)(2,1)S(1)} fusion(bf16[16,32,128]{1,0,2:T(8,128)(2,1)S(1)} %copy.30, bf16[512,32,128]{0,1,2:T(8,128)(2,1)} %copy.25), kind=kOutput, calls=%fused_computation.2 | convolution fusion | flops 68157440 | bytes 6422528 | tf_op jit(solution)/shard_map/ikh,jkh->ijh/dot_general | solution.py:61
  117.3 3.1 %copy.26 = bf16[16,512,128]{2,1,0:T(8,128)(2,1)} copy(bf16[16,512,128]{1,0,2:T(8,128)(2,1)S(1)} %convert_bitcast_fusion) | data formatting | bytes 4194304 | tf_op jit(solution)/shard_map/convert_element_type | solution.py:84
  120.4 2.1 %copy.28 = bf16[2,8,16,32,128]{4,3,2,1,0:T(8,128)(2,1)S(1)} copy(bf16[2,8,16,32,128]{4,3,0,1,2:T(8,128)(2,1)} %bitcast.38) | data formatting | bytes 4194304 | tf_op jit(solution)/shard_map/transpose | solution.py:34
  122.5 0.0 copy-start.4
  122.5 5.4 %all_to_all.10 = bf16[2,8,16,32,128]{4,3,2,1,0:T(8,128)(2,1)S(1)} all-to-all(bf16[2,8,16,32,128]{4,3,2,1,0:T(8,128)(2,1)S(1)} %copy.28), channel_id=1, replica_groups=mesh['rows_0'=2,'rows_1'=16,'ka_0'=2,'ka_1'=4,'ka_2'=2] {'ka_2'}, dimensions={0} | all-to-all | bytes 4194304 | tf_op jit(solution)/shard_map/all_to_all | solution.py:39
  128.0 1.7 %reduce_sum.61 = bf16[8,16,32,128]{3,2,1,0:T(8,128)(2,1)} reduce(bf16[2,8,16,32,128]{4,3,2,1,0:T(8,128)(2,1)S(1)} %all_to_all.10, bf16[]{:T(256)} %constant.14.clone.1), dimensions={0}, to_apply=%region_2.0 | reduce | flops 524288 | bytes 3145730 | tf_op jit(solution)/shard_map/reduce_sum | solution.py:40
  129.7 6.7 %all-to-all-start.1 = ((bf16[8,16,32,128]{3,2,1,0:T(8,128)(2,1)}), bf16[8,16,32,128]{3,2,1,0:T(8,128)(2,1)S(1)}, u32[]{:S(2)}, u32[]{:S(2)}) async-start(bf16[8,16,32,128]{3,2,1,0:T(8,128)(2,1)} %reduce_sum.61), calls=%async_computation.1 | async-start | bytes 2097152 | tf_op jit(solution)/shard_map/all_to_all | solution.py:47
  136.4 0.0 copy-done.4
  136.4 0.2 fusion.7
  136.6 15.6 %all-to-all-done.1 = bf16[8,16,32,128]{3,2,1,0:T(8,128)(2,1)S(1)} async-done(((bf16[8,16,32,128]{3,2,1,0:T(8,128)(2,1)}), bf16[8,16,32,128]{3,2,1,0:T(8,128)(2,1)S(1)}, u32[]{:S(2)}, u32[]{:S(2)}) %all-to-all-start.1) | async-done | bytes 1048608 | tf_op jit(solution)/shard_map/all_to_all | solution.py:47
  152.2 0.2 convert_reduce_fusion
  152.4 0.1 div.25
  152.5 0.3 multiply_reduce_fusion
  152.8 0.1 rsqrt.21
  152.9 0.2 fusion.18
  153.1 0.8 fusion.8
  (11 shorter events, 0.1 us)
Async XLA Ops:
  6.5 4.2 %copy-start = (bf16[128,256]{1,0:T(8,128)(2,1)S(1)}, bf16[128,256]{1,0:T(8,128)(2,1)}, u32[]{:S(2)}) copy-start(bf16[128,256]{1,0:T(8,128)(2,1)} %param.15) | copy-start | bytes 196612
  6.5 93.9 %all-gather.3.cloned.1.call-start = ((), (), s32[]{:S(2)}) async-start(), calls=%async_computation.2 | async-start | bytes 4456448 | tf_op jit(solution)/shard_map/all_gather | solution.py:20
  122.5 13.8 %copy-start.4 = (bf16[128,128]{1,0:T(8,128)(2,1)S(1)}, bf16[128,128]{1,0:T(8,128)(2,1)}, u32[]{:S(2)}) copy-start(bf16[128,128]{1,0:T(8,128)(2,1)} %param.16) | copy-start | bytes 98308
  128.0 24.9 %copy-start.2 = (f32[128]{0:T(128)S(1)}, f32[128]{0:T(128)}, u32[]{:S(2)}) copy-start(f32[128]{0:T(128)} %param.18) | copy-start | bytes 1540
  128.0 24.9 %copy-start.3 = (f32[128]{0:T(128)S(1)}, f32[128]{0:T(128)}, u32[]{:S(2)}) copy-start(f32[128]{0:T(128)} %param.17) | copy-start | bytes 1540
  128.0 25.1 %copy-start.1 = (bf16[128,128]{1,0:T(8,128)(2,1)S(1)}, bf16[128,128]{1,0:T(8,128)(2,1)}, u32[]{:S(2)}) copy-start(bf16[128,128]{1,0:T(8,128)(2,1)} %param.19) | copy-start | bytes 98308
  129.7 22.6 %all-to-all-start.1 = ((bf16[8,16,32,128]{3,2,1,0:T(8,128)(2,1)}), bf16[8,16,32,128]{3,2,1,0:T(8,128)(2,1)S(1)}, u32[]{:S(2)}, u32[]{:S(2)}) async-start(bf16[8,16,32,128]{3,2,1,0:T(8,128)(2,1)} %reduce_sum.61), calls=%async_computation.1 | async-start | bytes 2097152 | tf_op jit(solution)/shard_map/all_to_all | solution.py:47
Sparse Core Ops, SparseCore 0:
  18.3 82.0 all-gather.2
where the time goes:
time: 161 us
  waiting for transfers between devices  97.5 us (61%)
  local copies, waits for them, and re-layouts  20 us (12%)
  between operations  13.6 us (8%)
  blocking collectives  11.4 us (7%)
  starting transfers between devices  6.71 us (4%)
  other arithmetic  6.43 us (4%)
  matrix products  5.26 us (3%)
    all_gather x1, waiting for transfers between devices, stacked_from(): blocks = lax.all_gather(blocks, axes[k], axis=0, tiled=True)  81.8 us
    all_to_all x1, waiting for transfers between devices, sum_in_two_steps(): lax.all_to_all(nearer.astype(jnp.bfloat16), far, split_axis=0, concat_axi...  15.6 us
    another operation x1, local copies, waits for them, and re-layouts, joined_along(): blocks.reshape(*dims[:dim], dims[dim] * dims[dim + 1], *dims[dim + 2:])  8.64 us
    all_to_all x1, starting transfers between devices, sum_in_two_steps(): lax.all_to_all(nearer.astype(jnp.bfloat16), far, split_axis=0, concat_axi...  6.71 us
    all_gather x1, blocking collectives, stacked_from(): blocks = lax.all_gather(blocks, axes[k], axis=0, tiled=True)  6 us
    all_to_all x1, blocking collectives, sum_at_owner(): lax.all_to_all(blocks, axis, split_axis=0, concat_axis=0, tiled=True)  5.42 us
    transpose x1, local copies, waits for them, and re-layouts, stacked_from(): blocks.transpose(*turned, *range(len(order), blocks.ndim))  5.33 us
  transfers between devices with their start and end apart: 2, of which 2 were waited for; matrix products, arithmetic and copies ran while one was open for 0% of the time, Pallas kernels for 0%

commit v1 on v0

--- a/solution.py
+++ b/solution.py
@@ -6,6 +6,13 @@
 
 ROWS = ("rows_0", "rows_1")
 KA = ("ka_0", "ka_1", "ka_2")
+
+
+def exchange_gather(x, axis, d):
+    size = lax.axis_size(axis)
+    tiles = jnp.stack([x for _ in range(size)])
+    tiles = lax.all_to_all(tiles, axis, split_axis=0, concat_axis=0)
+    return jnp.concatenate(tiles, axis=d)
 
 
 def joined_along(blocks, dim):
@@ -17,7 +24,7 @@
 def stacked_from(array, axes, order):
     blocks = array[None]
     for k in order:
-        blocks = lax.all_gather(blocks, axes[k], axis=0, tiled=True)
+        blocks = exchange_gather(blocks, axes[k], 0)
     carried = [lax.axis_size(axes[k]) for k in reversed(order)]
     blocks = blocks.reshape(*carried, *array.shape)
     turned = sorted(range(len(order)), key=lambda place: order[len(order) - 1 - place])

time: 161 us -> 268 us (1.66)
  waiting for transfers between devices: 97.5 us -> 197 us
  starting transfers between devices: 6.71 us -> 22.3 us
  between operations: 13.6 us -> 0.17 us
  local copies, waits for them, and re-layouts: 20 us -> 22.9 us
    all_to_all x0 -> x1, waiting for transfers between devices: none -> 182 us  [exchange_gather(): tiles = lax.all_to_all(tiles, axis, split_axis=0, concat_axis=0)]
    all_gather x1 -> x0, waiting for transfers between devices: 81.8 us -> none  [stacked_from(): blocks = lax.all_gather(blocks, axes[k], axis=0, tiled=True)]
    all_to_all x0 -> x1, starting transfers between devices: none -> 15.2 us  [exchange_gather(): tiles = lax.all_to_all(tiles, axis, split_axis=0, concat_axis=0)]
    all_to_all x0 -> x1, blocking collectives: none -> 7.83 us  [exchange_gather(): tiles = lax.all_to_all(tiles, axis, split_axis=0, concat_axis=0)]
    all_gather x1 -> x0, blocking collectives: 6 us -> none  [stacked_from(): blocks = lax.all_gather(blocks, axes[k], axis=0, tiled=True)]
    all_to_all x0 -> x1, local copies, waits for them, and re-layouts: none -> 5.33 us  [exchange_gather(): tiles = lax.all_to_all(tiles, axis, split_axis=0, concat_axis=0)]
    transpose x1 -> x0, local copies, waits for them, and re-layouts: 5.33 us -> none  [stacked_from(): blocks.transpose(*turned, *range(len(order), blocks.ndim))]
    another operation x0 -> x2, local copies, waits for them, and re-layouts: none -> 2.96 us  [exchange_gather(): tiles = jnp.stack([x for _ in range(size)])]
where the time goes in v1:
time: 268 us
  waiting for transfers between devices  197 us (74%)
  local copies, waits for them, and re-layouts  22.9 us (9%)
  starting transfers between devices  22.3 us (8%)
  blocking collectives  13.3 us (5%)
  other arithmetic  6.45 us (2%)
  matrix products  5.26 us (2%)
    all_to_all x1, waiting for transfers between devices, exchange_gather(): tiles = lax.all_to_all(tiles, axis, split_axis=0, concat_axis=0)  182 us
    all_to_all x1, waiting for transfers between devices, sum_in_two_steps(): lax.all_to_all(nearer.astype(jnp.bfloat16), far, split_axis=0, concat_axi...  15.6 us
    all_to_all x1, starting transfers between devices, exchange_gather(): tiles = lax.all_to_all(tiles, axis, split_axis=0, concat_axis=0)  15.2 us
    another operation x1, local copies, waits for them, and re-layouts, joined_along(): blocks.reshape(*dims[:dim], dims[dim] * dims[dim + 1], *dims[dim + 2:])  8.64 us
    all_to_all x1, blocking collectives, exchange_gather(): tiles = lax.all_to_all(tiles, axis, split_axis=0, concat_axis=0)  7.83 us
    all_to_all x1, starting transfers between devices, sum_in_two_steps(): lax.all_to_all(nearer.astype(jnp.bfloat16), far, split_axis=0, concat_axi...  7.11 us
    all_to_all x1, blocking collectives, sum_at_owner(): lax.all_to_all(blocks, axis, split_axis=0, concat_axis=0, tiled=True)  5.42 us
  transfers between devices with their start and end apart: 2, of which 2 were waited for; matrix products, arithmetic and copies ran while one was open for 0% of the time, Pallas kernels for 0%

profile of v1, /device:TPU:32, one launch (start us, length us, event | category | flops | bytes accessed | tf_op | source)
XLA Modules:
  0.0 267.5 jit_solution(10425348278724128670)
XLA Ops:
  0.0 0.0 copy-start
  0.0 1.1 convert_reduce_fusion.2
  1.1 1.2 fusion.11
  2.3 0.7 convert_element_type.40
  3.0 0.1 convert_element_type.41
  3.1 1.1 fusion.14
  4.2 0.0 copy-done
  4.2 0.3 fusion.2
  4.5 1.1 fusion.4
  5.6 7.8 %all_to_all.20 = bf16[2,1,16,32,128]{4,3,2,1,0:T(8,128)(2,1)S(1)} all-to-all(bf16[2,1,16,32,128]{4,3,2,1,0:T(8,128)(2,1)S(1)} %pad_maximum_fusion), channel_id=1, replica_groups=mesh['rows_0'=2,'rows_1'=16,'ka_0'=2,'ka_1'=4,'ka_2'=2] {'rows_0'}, dimensions={0} | all-to-all | bytes 524288 | tf_op jit(solution)/shard_map/all_to_all | solution.py:14
  13.5 2.9 %stack.7 = bf16[16,2,16,32,128]{4,3,2,1,0:T(8,128)(2,1)} broadcast(bf16[2,16,32,128]{3,2,1,0:T(8,128)(2,1)S(1)} %bitcast.40), dimensions={1,2,3,4} | broadcast | bytes 4456448 | tf_op jit(solution)/shard_map/stack | solution.py:13
  16.4 15.2 %all-to-all-start.1 = ((bf16[16,2,16,32,128]{4,3,2,1,0:T(8,128)(2,1)}), bf16[16,2,16,32,128]{4,3,2,1,0:T(8,128)(2,1)}, u32[]{:S(2)}, u32[]{:S(2)}) async-start(bf16[16,2,16,32,128]{4,3,2,1,0:T(8,128)(2,1)} %stack.7), calls=%async_computation.1 | async-start | bytes 8388608 | tf_op jit(solution)/shard_map/all_to_all | solution.py:14
  31.6 0.4 copy.30
  32.0 181.6 %all-to-all-done.1 = bf16[16,2,16,32,128]{4,3,2,1,0:T(8,128)(2,1)} async-done(((bf16[16,2,16,32,128]{4,3,2,1,0:T(8,128)(2,1)}), bf16[16,2,16,32,128]{4,3,2,1,0:T(8,128)(2,1)}, u32[]{:S(2)}, u32[]{:S(2)}) %all-to-all-start.1) | async-done | bytes 4194336 | tf_op jit(solution)/shard_map/all_to_all | solution.py:14
  213.6 5.3 %copy.23 = bf16[16,2,16,32,128]{4,3,2,0,1:T(8,128)(2,1)} copy(bf16[16,2,16,32,128]{4,3,2,1,0:T(8,128)(2,1)} %all-to-all-done.1) | data formatting | bytes 8388608 | tf_op jit(solution)/shard_map/all_to_all | solution.py:14
  218.9 8.6 %copy.25 = bf16[512,32,128]{0,1,2:T(8,128)(2,1)} copy(bf16[512,32,128]{2,1,0:T(8,128)(2,1)} %bitcast.38) | data formatting | bytes 8388608 | tf_op jit(solution)/shard_map/reshape;reshape | solution.py:21
  227.6 2.9 %convert_bitcast_fusion = bf16[16,512,128]{1,0,2:T(8,128)(2,1)S(1)} fusion(bf16[16,32,128]{1,0,2:T(8,128)(2,1)S(1)} %copy.30, bf16[512,32,128]{0,1,2:T(8,128)(2,1)} %copy.25), kind=kOutput, calls=%fused_computation.2 | convolution fusion | flops 68157440 | bytes 6422528 | tf_op jit(solution)/shard_map/ikh,jkh->ijh/dot_general | solution.py:68
  230.5 3.1 %copy.26 = bf16[16,512,128]{2,1,0:T(8,128)(2,1)} copy(bf16[16,512,128]{1,0,2:T(8,128)(2,1)S(1)} %convert_bitcast_fusion) | data formatting | bytes 4194304 | tf_op jit(solution)/shard_map/convert_element_type | solution.py:91
  233.6 2.1 copy.28
  235.7 0.0 copy-start.4
  235.7 5.4 %all_to_all.21 = bf16[2,8,16,32,128]{4,3,2,1,0:T(8,128)(2,1)S(1)} all-to-all(bf16[2,8,16,32,128]{4,3,2,1,0:T(8,128)(2,1)S(1)} %copy.28), channel_id=1, replica_groups=mesh['rows_0'=2,'rows_1'=16,'ka_0'=2,'ka_1'=4,'ka_2'=2] {'ka_2'}, dimensions={0} | all-to-all | bytes 4194304 | tf_op jit(solution)/shard_map/all_to_all | solution.py:46
  241.2 1.7 reduce_sum.61
  242.8 7.1 %all-to-all-start.3 = ((bf16[8,16,32,128]{3,2,1,0:T(8,128)(2,1)}), bf16[8,16,32,128]{3,2,1,0:T(8,128)(2,1)S(1)}, u32[]{:S(2)}, u32[]{:S(2)}) async-start(bf16[8,16,32,128]{3,2,1,0:T(8,128)(2,1)} %reduce_sum.61), calls=%async_computation.3 | async-start | bytes 2097152 | tf_op jit(solution)/shard_map/all_to_all | solution.py:54
  250.0 0.2 fusion.7
  250.2 15.6 %all-to-all-done.3 = bf16[8,16,32,128]{3,2,1,0:T(8,128)(2,1)S(1)} async-done(((bf16[8,16,32,128]{3,2,1,0:T(8,128)(2,1)}), bf16[8,16,32,128]{3,2,1,0:T(8,128)(2,1)S(1)}, u32[]{:S(2)}, u32[]{:S(2)}) %all-to-all-start.3) | async-done | bytes 1048608 | tf_op jit(solution)/shard_map/all_to_all | solution.py:54
  265.8 0.2 convert_reduce_fusion
  266.0 0.1 div.25
  266.1 0.3 multiply_reduce_fusion
  266.4 0.1 rsqrt.21
  266.5 0.0 copy-done.2
  266.5 0.2 fusion.18
  266.7 0.8 fusion.8
  (12 shorter events, 0.1 us)
Async XLA Ops:
  0.0 4.2 %copy-start = (bf16[128,256]{1,0:T(8,128)(2,1)S(1)}, bf16[128,256]{1,0:T(8,128)(2,1)}, u32[]{:S(2)}) copy-start(bf16[128,256]{1,0:T(8,128)(2,1)} %param.15) | copy-start | bytes 196612
  16.4 197.2 %all-to-all-start.1 = ((bf16[16,2,16,32,128]{4,3,2,1,0:T(8,128)(2,1)}), bf16[16,2,16,32,128]{4,3,2,1,0:T(8,128)(2,1)}, u32[]{:S(2)}, u32[]{:S(2)}) async-start(bf16[16,2,16,32,128]{4,3,2,1,0:T(8,128)(2,1)} %stack.7), calls=%async_computation.1 | async-start | bytes 8388608 | tf_op jit(solution)/shard_map/all_to_all | solution.py:14
  235.7 14.2 %copy-start.4 = (bf16[128,128]{1,0:T(8,128)(2,1)S(1)}, bf16[128,128]{1,0:T(8,128)(2,1)}, u32[]{:S(2)}) copy-start(bf16[128,128]{1,0:T(8,128)(2,1)} %param.16) | copy-start | bytes 98308
  241.2 25.3 %copy-start.2 = (f32[128]{0:T(128)S(1)}, f32[128]{0:T(128)}, u32[]{:S(2)}) copy-start(f32[128]{0:T(128)} %param.18) | copy-start | bytes 1540
  241.2 25.3 %copy-start.3 = (f32[128]{0:T(128)S(1)}, f32[128]{0:T(128)}, u32[]{:S(2)}) copy-start(f32[128]{0:T(128)} %param.17) | copy-start | bytes 1540
  241.2 25.5 %copy-start.1 = (bf16[128,128]{1,0:T(8,128)(2,1)S(1)}, bf16[128,128]{1,0:T(8,128)(2,1)}, u32[]{:S(2)}) copy-start(bf16[128,128]{1,0:T(8,128)(2,1)} %param.19) | copy-start | bytes 98308
  242.8 23.0 %all-to-all-start.3 = ((bf16[8,16,32,128]{3,2,1,0:T(8,128)(2,1)}), bf16[8,16,32,128]{3,2,1,0:T(8,128)(2,1)S(1)}, u32[]{:S(2)}, u32[]{:S(2)}) async-start(bf16[8,16,32,128]{3,2,1,0:T(8,128)(2,1)} %reduce_sum.61), calls=%async_computation.3 | async-start | bytes 2097152 | tf_op jit(solution)/shard_map/all_to_all | solution.py:54
